TPU v7x, 8 devices: a whole 2x2x1 slice. The times are simulated.
8 devices in a mesh: rep: 1 (over z), head: 2 (over y), seq: 4 (over x, core).
Axes of the slice: x: 2, y: 2, z: 1, core: 2. Of those that a mesh axis runs over, the one named last changes fastest.
Arguments:
- tokens: bfloat16 [32, 3072], P('rep')
- w_query: bfloat16 [3072, 4096], replicated
- w_key: bfloat16 [3072, 4096], replicated
- w_value: bfloat16 [3072, 4096], replicated
- w_out: bfloat16 [4096, 3072], P(('head', 'seq'))
- k_cache: bfloat16 [32, 1024, 16, 256], P('rep', 'seq', 'head')
- v_cache: bfloat16 [32, 1024, 16, 256], P('rep', 'seq', 'head')
- positions: int32 [32], P('rep')
Outputs:
- output 1: bfloat16 [32, 3072], P('rep')
- output 2: bfloat16 [32, 1024, 16, 256], P('rep', 'seq', 'head')
- output 3: bfloat16 [32, 1024, 16, 256], P('rep', 'seq', 'head')
All inputs are finite; a program needn't handle non-finite values.
Results may differ from a plain program's by a relative error of at most 0.00595572.
Values are sent between devices in bfloat16 or wider.
A program may use at most 1 GiB of HBM per device.

v0:
```python
import functools

import jax
import jax.numpy as jnp
from jax import lax
from jax.experimental import pallas as pl
from jax.experimental.pallas import tpu as pltpu
from jax.sharding import PartitionSpec as P

MESH = pl.DeviceIdType.MESH
RING = 6
AHEAD = 4
HELD = 4
PARTS = 4
F32 = jnp.float32
BF16 = jnp.bfloat16
NT = (((1,), (1,)), ((), ()))


def _at(h, s):
    return {"head": h, "seq": s}


def _greet(peers):
    barrier = pltpu.get_barrier_semaphore()
    for peer in peers:
        pl.semaphore_signal(barrier, inc=1, device_id=peer, device_id_type=MESH)
    return lambda: pl.semaphore_wait(barrier, len(peers))


def project_kernel(x_hbm, wq_ref, wk_ref, wv_ref, k_hbm, v_hbm,
                   qkv_ref, kring, vring,
                   x_ref, wbuf, held, xsem, wsem, ringsem, ssem, rsem):
    nseq = held.shape[0]
    h, s = lax.axis_index("head"), lax.axis_index("seq")
    cols = wbuf.shape[-1]
    rows = wbuf.shape[2]
    first = pl.multiple_of((h * nseq + s) * cols, 128)
    peers = [lax.rem(s + d, nseq) for d in range(1, nseq)]
    joined = _greet([_at(h, p) for p in peers])
    tokens = pltpu.make_async_copy(x_hbm, x_ref, xsem)
    tokens.start()
    loads = []
    for j, w in enumerate((wq_ref, wk_ref, wv_ref)):
        for p in range(PARTS):
            c = pltpu.make_async_copy(
                w.at[pl.ds(p * rows, rows), pl.ds(first, cols)], wbuf.at[j, p], wsem.at[j, p])
            c.start()
            loads.append(c)
    ring = []
    for b in range(AHEAD):
        for i, (src, dst) in enumerate(((k_hbm, kring), (v_hbm, vring))):
            pair = pl.ds(2 * b, 2)
            ring.append(pltpu.make_async_copy(src.at[pair], dst.at[pair], ringsem.at[i, b]))
    asked = 0
    sends = []
    tokens.wait()
    for j in range(3):
        acc = None
        for p in range(PARTS):
            loads[j * PARTS + p].wait()
            share = -(-len(ring) * (j * PARTS + p + 1) // (3 * PARTS))
            while asked < share:
                ring[asked].start()
                asked += 1
            part = jnp.dot(x_ref[:, p * rows:(p + 1) * rows], wbuf[j, p], preferred_element_type=F32)
            acc = part if acc is None else acc + part
        held[s, j] = acc.astype(BF16)
        if j == 0:
            joined()
        for i, p in enumerate(peers):
            c = pltpu.make_async_remote_copy(
                src_ref=held.at[s, j], dst_ref=held.at[s, j], send_sem=ssem.at[j, i], recv_sem=rsem.at[j, i],
                device_id=_at(h, p), device_id_type=MESH)
            c.start()
            sends.append(c)

    def spread(src, which):
        per = cols // 256
        for j in which:
            for i in range(per):
                for half in range(2):
                    val = held[src, j, :, i * 256 + half * 128:i * 256 + half * 128 + 128].astype(F32)
                    qkv_ref[j, half, pl.ds(src * per + i, val.shape[0], stride=nseq * per), :] = val

    spread(s, range(3))
    for j in range(3):
        for i in range(nseq - 1):
            sends[j * (nseq - 1) + i].wait_recv()
            spread(lax.rem(s + nseq - 1 - i, nseq), (j,))
    for c in sends:
        c.wait_send()
    for c in ring:
        c.wait()


def attend_kernel(scale, pos_ref, qkv_ref, k_hbm, v_hbm, kring_in, vring_in,
                  ko_hbm, vo_hbm, kring, vring, *rest):
    chunks = rest[:-7]
    obuf, mbuf, lbuf, kin, vin, kout, vout = rest[-7:]
    batch, wide, hd = k_hbm.shape
    nseq = len(chunks)
    heads = obuf.shape[1] // batch
    per = heads // nseq
    span = wide // heads
    pairs = batch // 2
    base = lax.axis_index("seq") * span
    col = lax.broadcasted_iota(jnp.int32, (heads, wide), 1)
    row = lax.broadcasted_iota(jnp.int32, (heads, wide), 0)
    own = lax.rem(col, heads) == row
    slot_of = jnp.where(own, base + col // heads, batch * nseq * span)

    def both(i):
        return pl.ds(pl.multiple_of(i * 2, 2), 2)

    def reads(i):
        slot = lax.rem(i, RING)
        return [pltpu.make_async_copy(src.at[both(i)], dst.at[both(slot)], sem.at[slot])
                for src, dst, sem in ((k_hbm, kring, kin), (v_hbm, vring, vin))]

    def writes(i):
        slot = lax.rem(i, RING)
        return [pltpu.make_async_copy(src.at[both(slot)], dst.at[both(i)], sem.at[slot])
                for src, dst, sem in ((kring, ko_hbm, kout), (vring, vo_hbm, vout))]

    def fresh(j, lines):
        return jnp.concatenate([qkv_ref[j, 0, lines, :], qkv_ref[j, 1, lines, :]], axis=-1).astype(BF16)

    def body(i, carry):
        nxt = i + AHEAD

        @pl.when(nxt < pairs)
        def _():
            @pl.when(nxt >= RING)
            def _():
                for c in writes(nxt - RING):
                    c.wait()

            for c in reads(nxt):
                c.start()

        @pl.when(i >= AHEAD)
        def _():
            for c in reads(i):
                c.wait()

        rows = []
        for g in range(2):
            b = 2 * i + g
            pos = pos_ref[b]
            at = pos - base
            lines = pl.ds(pl.multiple_of(b * heads, heads), heads)
            spot = pl.ds(pl.multiple_of(at * heads, heads), heads)
            ks = 2 * lax.rem(i, RING) + g

            @pl.when(jnp.logical_and(at >= 0, at < span))
            def _():
                kring[ks, spot, :] = fresh(1, lines)
                vring[ks, spot, :] = fresh(2, lines)

            rows.append((b, pos, lines, ks))
        scores = []
        for b, pos, lines, ks in rows:
            score = lax.dot_general(fresh(0, lines), kring[ks], NT, preferred_element_type=F32) * scale
            scores.append(jnp.where(slot_of <= pos, score, -jnp.inf))
        for (b, pos, lines, ks), score in zip(rows, scores):
            top = jnp.max(score, axis=-1, keepdims=True)
            safe = jnp.where(top == -jnp.inf, 0.0, top)
            weight = jnp.exp(score - safe)
            total = jnp.sum(weight, axis=-1, keepdims=True)
            mix = jnp.dot(weight.astype(BF16), vring[ks], preferred_element_type=F32)
            obuf[0, lines, :] = mix[:, :128]
            obuf[1, lines, :] = mix[:, 128:]
            mbuf[lines, :] = jnp.broadcast_to(top, (heads, 128))
            lbuf[lines, :] = jnp.broadcast_to(total, (heads, 128))

        @pl.when(i < pairs - HELD)
        def _():
            for c in writes(i):
                c.start()

        return carry

    lax.fori_loop(0, pairs, body, 0)
    eye = (lax.broadcasted_iota(jnp.int32, (batch, 128), 0)
           == lax.broadcasted_iota(jnp.int32, (batch, 128), 1))
    me = lax.axis_index("seq")
    for d, chunk in enumerate(chunks):
        for e in range(per):
            pick = pl.ds(jnp.bitwise_xor(me, d) * per + e, batch, stride=heads)
            rows = slice(e * batch, (e + 1) * batch)
            chunk[rows, :128] = obuf[0, pick, :]
            chunk[rows, 128:] = obuf[1, pick, :]
            for i, buf in enumerate((mbuf, lbuf)):
                line = per * batch + 2 * e + i
                chunk[line:line + 1, :128] = jnp.sum(jnp.where(eye, buf[pick, :], 0.0), axis=0, keepdims=True)
                chunk[line:line + 1, 128:] = jnp.zeros((1, hd - 128), F32)
        used = per * batch + 2 * per
        chunk[used:, :] = jnp.zeros((chunk.shape[0] - used, hd), F32)
    for i in range(pairs - RING, pairs - HELD):
        for c in writes(i):
            c.wait()


def write_kernel(kring, vring, ko_in, vo_in, chunk, ko_hbm, vo_hbm, done, sem):
    pairs = ko_hbm.shape[0] // 2
    copies = []
    for i in range(pairs - HELD, pairs):
        for src, dst in ((kring, ko_hbm), (vring, vo_hbm)):
            c = pltpu.make_async_copy(
                src.at[pl.ds(i % RING * 2, 2)], dst.at[pl.ds(i * 2, 2)], sem.at[len(copies)])
            c.start()
            copies.append(c)
    done[...] = jnp.zeros_like(done)
    for c in copies:
        c.wait()


def finish_kernel(*refs):
    got = refs[:-10]
    wo, after, y_ref, ysend, ygot, yout, s2, r2, s3, r3 = refs[-10:]
    nseq = len(got)
    ndev, batch, cols = ysend.shape
    hd = got[0].shape[1]
    per = (got[0].shape[0] - 8) // batch
    h, s = lax.axis_index("head"), lax.axis_index("seq")
    me = h * nseq + s
    far = [lax.rem(me + d, ndev) for d in range(1, ndev)]
    joined = _greet([_at(p // nseq, lax.rem(p, nseq)) for p in far])
    eye = (lax.broadcasted_iota(jnp.int32, (batch, hd), 0)
           == lax.broadcasted_iota(jnp.int32, (batch, hd), 1))
    y = None
    for e in range(per):
        line = per * batch + 2 * e
        tops = [got[i][line:line + 1, :] for i in range(nseq)]
        sums = [got[i][line + 1:line + 2, :] for i in range(nseq)]
        top = functools.reduce(jnp.maximum, tops)
        mix, total = None, None
        for i in range(nseq):
            factor = jnp.exp(tops[i] - top)
            share = factor * sums[i]
            total = share if total is None else total + share
            down = jnp.sum(jnp.where(eye, factor, 0.0), axis=1, keepdims=True)
            term = got[i][e * batch:(e + 1) * batch, :] * down
            mix = term if mix is None else mix + term
        down = jnp.sum(jnp.where(eye, total, 0.0), axis=1, keepdims=True)
        attn = (mix / down).astype(BF16)
        term = jnp.dot(attn, wo[e * hd:(e + 1) * hd, :], preferred_element_type=F32)
        y = term if y is None else y + term
    for p in range(ndev):
        ysend[p] = y[:, p * cols:(p + 1) * cols]
    joined()
    moves = []
    for i, p in enumerate(far):
        c = pltpu.make_async_remote_copy(
            src_ref=ysend.at[p], dst_ref=ygot.at[i], send_sem=s2.at[i], recv_sem=r2.at[i],
            device_id=_at(p // nseq, lax.rem(p, nseq)), device_id_type=MESH)
        c.start()
        moves.append(c)
    acc = ysend[me]
    for i, c in enumerate(moves):
        c.wait_recv()
        acc = acc + ygot[i]
    yout[me] = acc.astype(BF16)
    shares = []
    for i, p in enumerate(far):
        c = pltpu.make_async_remote_copy(
            src_ref=yout.at[me], dst_ref=yout.at[me], send_sem=s3.at[i], recv_sem=r3.at[i],
            device_id=_at(p // nseq, lax.rem(p, nseq)), device_id_type=MESH)
        c.start()
        shares.append(c)
    for c in shares:
        c.wait_recv()
    for p in range(ndev):
        y_ref[:, p * cols:(p + 1) * cols] = yout[p]
    for c in moves + shares:
        c.wait_send()


def solution(mesh):
    nhead, nseq = mesh.shape["head"], mesh.shape["seq"]
    ndev = nhead * nseq
    cache_spec = P("rep", "seq", "head", None)
    any_spec = pl.BlockSpec(memory_space=pl.ANY)
    vmem = pl.BlockSpec(memory_space=pltpu.VMEM)
    smem = pl.BlockSpec(memory_space=pltpu.SMEM)

    def local_step(tokens, w_query, w_key, w_value, w_out, k_cache, v_cache, positions):
        batch, span, heads, hd = k_cache.shape
        model = tokens.shape[1]
        cols = heads * hd // nseq
        per = heads // nseq
        cache = jax.ShapeDtypeStruct((batch, span * heads, hd), BF16)
        ring = jax.ShapeDtypeStruct((2 * RING, span * heads, hd), BF16)
        k_flat, v_flat = k_cache.reshape(cache.shape), v_cache.reshape(cache.shape)
        dma = pltpu.SemaphoreType.DMA
        qkv, kring, vring = pl.pallas_call(
            project_kernel,
            out_shape=(jax.ShapeDtypeStruct((3, 2, batch * heads, 128), F32), ring, ring),
            in_specs=[pl.BlockSpec(memory_space=pltpu.HBM)] + [any_spec] * 5,
            out_specs=(vmem, vmem, vmem),
            scratch_shapes=[
                pltpu.VMEM(tokens.shape, BF16),
                pltpu.VMEM((3, PARTS, model // PARTS, cols), BF16),
                pltpu.VMEM((nseq, 3, batch, cols), BF16),
                dma, dma((3, PARTS)), dma((2, AHEAD)), dma((3, nseq - 1)), dma((3, nseq - 1)),
            ],
            compiler_params=pltpu.CompilerParams(
                collective_id=0, has_side_effects=True, vmem_limit_bytes=11 * 2**20),
        )(tokens, w_query, w_key, w_value, k_flat, v_flat)
        chunk = jax.ShapeDtypeStruct((per * batch + 8, hd), F32)
        chunk = jax.ShapeDtypeStruct((per * batch + 8, hd), F32)
        k_out, v_out, kring, vring, *chunks = pl.pallas_call(
            functools.partial(attend_kernel, hd ** -0.5),
            out_shape=(cache, cache, ring, ring) + (chunk,) * nseq,
            in_specs=[smem, vmem, any_spec, any_spec, vmem, vmem],
            out_specs=(any_spec, any_spec, vmem, vmem) + (vmem,) * nseq,
            input_output_aliases={4: 2, 5: 3},
            scratch_shapes=[
                pltpu.VMEM((2, batch * heads, 128), F32),
                pltpu.VMEM((batch * heads, 128), F32),
                pltpu.VMEM((batch * heads, 128), F32),
                dma((RING,)), dma((RING,)), dma((RING,)), dma((RING,)),
            ],
            compiler_params=pltpu.CompilerParams(vmem_limit_bytes=4 * 2**20),
        )(positions, qkv, k_flat, v_flat, kring, vring)
        got = [lax.ppermute(chunks[d], "seq", [(i, i ^ d) for i in range(nseq)]) for d in range(1, nseq)]
        k_out, v_out, after = pl.pallas_call(
            write_kernel,
            out_shape=(cache, cache, jax.ShapeDtypeStruct((8, 128), F32)),
            in_specs=[vmem, vmem, any_spec, any_spec, vmem],
            out_specs=(any_spec, any_spec, vmem),
            input_output_aliases={2: 0, 3: 1},
            scratch_shapes=[dma((2 * HELD,))],
            compiler_params=pltpu.CompilerParams(vmem_limit_bytes=1 * 2**20),
            cost_estimate=pl.CostEstimate(flops=10**9, bytes_accessed=8 * HELD * 2**20, transcendentals=0),
        )(kring, vring, k_out, v_out, chunks[0])
        ycols = model // ndev
        y = pl.pallas_call(
            finish_kernel,
            out_shape=jax.ShapeDtypeStruct((batch, model), BF16),
            in_specs=[vmem] * (nseq + 2),
            out_specs=vmem,
            scratch_shapes=[
                pltpu.VMEM((ndev, batch, ycols), F32),
                pltpu.VMEM((ndev, batch, ycols), F32),
                pltpu.VMEM((ndev, batch, ycols), BF16),
                dma((ndev,)), dma((ndev,)), dma((ndev,)), dma((ndev,)),
            ],
            compiler_params=pltpu.CompilerParams(
                collective_id=1, has_side_effects=True, vmem_limit_bytes=6 * 2**20),
        )(chunks[0], *got, w_out, after)
        return y, k_out.reshape(k_cache.shape), v_out.reshape(v_cache.shape)

    return jax.shard_map(
        local_step,
        mesh=mesh,
        in_specs=(P("rep", None), P(), P(), P(), P(("head", "seq"), None), cache_spec, cache_spec, P("rep")),
        out_specs=(P("rep", None), cache_spec, cache_spec),
        check_vma=False,
    )
```

profile of v0, /device:TPU:0, one launch (start us, length us, event | category | flops | bytes accessed | tf_op | source)
XLA Modules:
  0.0 69.2 jit_solution(13401743715960540073)
XLA Ops:
  0.6 0.0 copy-start.1
  0.6 0.9 %copy-done.1 = bf16[32,3072]{1,0:T(8,128)(2,1)S(1)} copy-done((bf16[32,3072]{1,0:T(8,128)(2,1)S(1)}, bf16[32,3072]{1,0:T(8,128)(2,1)}, u32[]{:S(2)}) %copy-start.1) | copy-done | bytes 196632
  1.6 0.0 copy-start.2
  1.6 10.8 %shard_map.103 = (f32[3,2,256,128]{3,2,1,0:T(8,128)S(1)}, bf16[12,2048,256]{2,1,0:T(8,128)(2,1)S(1)}, bf16[12,2048,256]{2,1,0:T(8,128)(2,1)S(1)}) custom-call(bf16[32,3072]{1,0:T(8,128)(2,1)S(1)} %copy-done.1, bf16[3072,4096]{1,0:T(8,128)(2,1)} %wq_ref.1, bf16[3072,4096]{1,0:T(8,128)(2,1)} %wk_ref.1, bf16[3072,4096]{1,0:T(8,128)(2,1)} %wv_ref.1, ...), custom_call_target="tpu_custom_call" | custom-call | tf_op jit(solution)/shard_map/pallas_call | solution.py:297
  12.3 0.0 copy-done.2
  12.4 34.7 %shard_map.104 = (bf16[32,2048,256]{2,1,0:T(8,128)(2,1)}, bf16[32,2048,256]{2,1,0:T(8,128)(2,1)}, bf16[12,2048,256]{2,1,0:T(8,128)(2,1)S(1)}, bf16[12,2048,256]{...) custom-call(s32[32]{0:T(128)S(1)} %copy-done.2, ...), custom_call_target="tpu_custom_call", output_to_operand_aliasing={{2}: (4, {}), {3}: (5, {})} | custom-call | tf_op jit(solution)/shard_map/pallas_call | solution.py:313
  47.0 0.2 collective-permute-start
  47.2 1.8 %collective-permute-start.1 = (f32[72,256]{1,0:T(8,128)S(1)}, f32[72,256]{1,0:T(8,128)S(1)}, u32[]{:S(2)}, u32[]{:S(2)}) collective-permute-start(f32[72,256]{1,0:T(8,128)S(1)} %get-tuple-element.22), channel_id=1, source_target_pairs={{0,2},{1,3},{2,0},{3,1},{4,6},{5,7},{6,4},{7,5}} | collective-permute-start | bytes 221192 | tf_op jit(solution)/shard_map/ppermute | solution.py:327
  49.0 0.1 collective-permute-start.2
  49.1 0.0 copy-start
  49.1 6.4 %shard_map.105 = (bf16[32,2048,256]{2,1,0:T(8,128)(2,1)}, bf16[32,2048,256]{2,1,0:T(8,128)(2,1)}, f32[8,128]{1,0:T(8,128)S(1)}) custom-call(bf16[12,2048,256]{2,1,0:T(8,128)(2,1)S(1)} %get-tuple-element.24.kring, bf16[12,2048,256]{2,1,0:T(8,128)(2,1)S(1)} %get-tuple-element.25.vring, ...), custom_call_target="tpu_custom_call", output_to_operand_aliasing={{0}: (2, {}), {1}: (3, {})} | custom-call | flops 1000000000 | bytes 33554432 | tf_op jit(solution)/shard_map/pallas_call | solution.py:328
  55.5 0.0 collective-permute-done.refs_1_
  55.5 0.0 collective-permute-done.1.refs_2_
  55.5 0.0 collective-permute-done.2.refs_3_
  55.5 0.0 copy-done
  55.5 13.0 %shard_map.106 = bf16[32,3072]{1,0:T(8,128)(2,1)S(1)} custom-call(f32[72,256]{1,0:T(8,128)S(1)} %get-tuple-element.20.chunk.refs_0_, f32[72,256]{1,0:T(8,128)S(1)} %collective-permute-done.refs_1_, f32[72,256]{1,0:T(8,128)S(1)} %collective-permute-done.1.refs_2_, f32[72,256]{1,0:T(8,128)S(1)} %collective-permute-done.2.refs_3_, ...), custom_call_target="tpu_custom_call" | custom-call | tf_op jit(solution)/shard_map/pallas_call | solution.py:339
  68.5 0.7 copy.20
Async XLA Ops:
  0.6 0.9 %copy-start.1 = (bf16[32,3072]{1,0:T(8,128)(2,1)S(1)}, bf16[32,3072]{1,0:T(8,128)(2,1)}, u32[]{:S(2)}) copy-start(bf16[32,3072]{1,0:T(8,128)(2,1)} %x_hbm.1) | copy-start | bytes 589828
  1.6 10.8 %copy-start.2 = (s32[32]{0:T(128)S(1)}, s32[32]{0:T(128)}, u32[]{:S(2)}) copy-start(s32[32]{0:T(128)} %pos_ref.1) | copy-start | bytes 388
  47.0 8.5 %collective-permute-start = (f32[72,256]{1,0:T(8,128)S(1)}, f32[72,256]{1,0:T(8,128)S(1)}, u32[]{:S(2)}, u32[]{:S(2)}) collective-permute-start(f32[72,256]{1,0:T(8,128)S(1)} %get-tuple-element.21), channel_id=1, source_target_pairs={{0,1},{1,0},{2,3},{3,2},{4,5},{5,4},{6,7},{7,6}} | collective-permute-start | bytes 221192 | tf_op jit(solution)/shard_map/ppermute | solution.py:327
  47.2 8.3 %collective-permute-start.1 = (f32[72,256]{1,0:T(8,128)S(1)}, f32[72,256]{1,0:T(8,128)S(1)}, u32[]{:S(2)}, u32[]{:S(2)}) collective-permute-start(f32[72,256]{1,0:T(8,128)S(1)} %get-tuple-element.22), channel_id=1, source_target_pairs={{0,2},{1,3},{2,0},{3,1},{4,6},{5,7},{6,4},{7,5}} | collective-permute-start | bytes 221192 | tf_op jit(solution)/shard_map/ppermute | solution.py:327
  49.0 6.5 %collective-permute-start.2 = (f32[72,256]{1,0:T(8,128)S(1)}, f32[72,256]{1,0:T(8,128)S(1)}, u32[]{:S(2)}, u32[]{:S(2)}) collective-permute-start(f32[72,256]{1,0:T(8,128)S(1)} %get-tuple-element.23), channel_id=1, source_target_pairs={{0,3},{1,2},{2,1},{3,0},{4,7},{5,6},{6,5},{7,4}} | collective-permute-start | bytes 221192 | tf_op jit(solution)/shard_map/ppermute | solution.py:327
  49.1 6.4 %copy-start = (bf16[512,3072]{1,0:T(8,128)(2,1)S(1)}, bf16[512,3072]{1,0:T(8,128)(2,1)}, u32[]{:S(2)}) copy-start(bf16[512,3072]{1,0:T(8,128)(2,1)} %refs_4_.1) | copy-start | bytes 9437188
where the time goes:
time: 69.3 us; the launch traced here: 69.2 us
  Pallas kernels  64.8 us (94%)
  starting transfers between devices  2.07 us (3%)
  local copies, waits for them, and re-layouts  1.61 us (2%)
  between operations  0.71 us (1%)
    pallas_call x1, Pallas kernels, local_step(): pl.pallas_call(functools.partial(attend_kernel, hd ** (-0.5)), out_shape=...  34.7 us
    pallas_call x1, Pallas kernels, local_step(): pl.pallas_call(finish_kernel, out_shape=jax.ShapeDtypeStruct((batch, mode...  13 us
    pallas_call x1, Pallas kernels, local_step(): pl.pallas_call(project_kernel, out_shape=(jax.ShapeDtypeStruct((3, 2, bat...  10.8 us
    pallas_call x1, Pallas kernels, local_step(): pl.pallas_call(write_kernel, out_shape=(cache, cache, jax.ShapeDtypeStruc...  6.39 us
    ppermute x3, starting transfers between devices, local_step(): lax.ppermute(chunks[d], 'seq', [(i, i ^ d) for i in range(nseq)])  2.07 us
    unnamed x7, local copies, waits for them, and re-layouts  1.61 us
  transfers between devices with their start and end apart: 3, of which 0 were waited for; matrix products, arithmetic and copies ran while one was open for 0% of the time, Pallas kernels for 9%

commit v1 on v0

--- a/solution.py
+++ b/solution.py
@@ -8,9 +8,9 @@
 from jax.sharding import PartitionSpec as P
 
 MESH = pl.DeviceIdType.MESH
-RING = 6
-AHEAD = 4
+RING = 8
 HELD = 4
+AHEAD = 2
 PARTS = 4
 F32 = jnp.float32
 BF16 = jnp.bfloat16
@@ -19,6 +19,13 @@
 
 def _at(h, s):
     return {"head": h, "seq": s}
+
+
+def _flip(a, bits):
+    for bit in (1, 2, 4):
+        if bits & bit:
+            a = a + bit * (1 - 2 * lax.rem(a // bit, 2))
+    return a
 
 
 def _greet(peers):
@@ -48,7 +55,7 @@
             c.start()
             loads.append(c)
     ring = []
-    for b in range(AHEAD):
+    for b in range(HELD):
         for i, (src, dst) in enumerate(((k_hbm, kring), (v_hbm, vring))):
             pair = pl.ds(2 * b, 2)
             ring.append(pltpu.make_async_copy(src.at[pair], dst.at[pair], ringsem.at[i, b]))
@@ -113,33 +120,39 @@
     def both(i):
         return pl.ds(pl.multiple_of(i * 2, 2), 2)
 
+    flow = RING - HELD
+
+    def place(i):
+        return HELD + lax.rem(i - HELD, flow)
+
     def reads(i):
-        slot = lax.rem(i, RING)
+        slot = place(i)
         return [pltpu.make_async_copy(src.at[both(i)], dst.at[both(slot)], sem.at[slot])
                 for src, dst, sem in ((k_hbm, kring, kin), (v_hbm, vring, vin))]
 
     def writes(i):
-        slot = lax.rem(i, RING)
+        slot = place(i)
         return [pltpu.make_async_copy(src.at[both(slot)], dst.at[both(i)], sem.at[slot])
                 for src, dst, sem in ((kring, ko_hbm, kout), (vring, vo_hbm, vout))]
 
     def fresh(j, lines):
         return jnp.concatenate([qkv_ref[j, 0, lines, :], qkv_ref[j, 1, lines, :]], axis=-1).astype(BF16)
 
+    for i in range(HELD, HELD + flow):
+        for c in reads(i):
+            c.start()
+
     def body(i, carry):
         nxt = i + AHEAD
 
-        @pl.when(nxt < pairs)
+        @pl.when(jnp.logical_and(nxt >= RING, nxt < pairs))
         def _():
-            @pl.when(nxt >= RING)
-            def _():
-                for c in writes(nxt - RING):
-                    c.wait()
-
+            for c in writes(nxt - flow):
+                c.wait()
             for c in reads(nxt):
                 c.start()
 
-        @pl.when(i >= AHEAD)
+        @pl.when(i >= HELD)
         def _():
             for c in reads(i):
                 c.wait()
@@ -151,7 +164,7 @@
             at = pos - base
             lines = pl.ds(pl.multiple_of(b * heads, heads), heads)
             spot = pl.ds(pl.multiple_of(at * heads, heads), heads)
-            ks = 2 * lax.rem(i, RING) + g
+            ks = 2 * jnp.where(i < HELD, i, place(jnp.maximum(i, HELD))) + g
 
             @pl.when(jnp.logical_and(at >= 0, at < span))
             def _():
@@ -174,7 +187,7 @@
             mbuf[lines, :] = jnp.broadcast_to(top, (heads, 128))
             lbuf[lines, :] = jnp.broadcast_to(total, (heads, 128))
 
-        @pl.when(i < pairs - HELD)
+        @pl.when(i >= HELD)
         def _():
             for c in writes(i):
                 c.start()
@@ -187,7 +200,7 @@
     me = lax.axis_index("seq")
     for d, chunk in enumerate(chunks):
         for e in range(per):
-            pick = pl.ds(jnp.bitwise_xor(me, d) * per + e, batch, stride=heads)
+            pick = pl.ds(_flip(me, d) * per + e, batch, stride=heads)
             rows = slice(e * batch, (e + 1) * batch)
             chunk[rows, :128] = obuf[0, pick, :]
             chunk[rows, 128:] = obuf[1, pick, :]
@@ -197,18 +210,17 @@
                 chunk[line:line + 1, 128:] = jnp.zeros((1, hd - 128), F32)
         used = per * batch + 2 * per
         chunk[used:, :] = jnp.zeros((chunk.shape[0] - used, hd), F32)
-    for i in range(pairs - RING, pairs - HELD):
+    for i in range(pairs - flow, pairs):
         for c in writes(i):
             c.wait()
 
 
 def write_kernel(kring, vring, ko_in, vo_in, chunk, ko_hbm, vo_hbm, done, sem):
-    pairs = ko_hbm.shape[0] // 2
     copies = []
-    for i in range(pairs - HELD, pairs):
+    for i in range(HELD):
         for src, dst in ((kring, ko_hbm), (vring, vo_hbm)):
-            c = pltpu.make_async_copy(
-                src.at[pl.ds(i % RING * 2, 2)], dst.at[pl.ds(i * 2, 2)], sem.at[len(copies)])
+            pair = pl.ds(i * 2, 2)
+            c = pltpu.make_async_copy(src.at[pair], dst.at[pair], sem.at[len(copies)])
             c.start()
             copies.append(c)
     done[...] = jnp.zeros_like(done)
@@ -217,19 +229,25 @@
 
 
 def finish_kernel(*refs):
-    got = refs[:-10]
-    wo, after, y_ref, ysend, ygot, yout, s2, r2, s3, r3 = refs[-10:]
+    got = refs[:-14]
+    wo, after, y_ref, theirs, ours, half, ygot, yout, s1, r1, s2, r2, s3, r3 = refs[-14:]
     nseq = len(got)
-    ndev, batch, cols = ysend.shape
+    chips, batch, cols = ours.shape
+    ndev = 2 * chips
     hd = got[0].shape[1]
     per = (got[0].shape[0] - 8) // batch
     h, s = lax.axis_index("head"), lax.axis_index("seq")
     me = h * nseq + s
-    far = [lax.rem(me + d, ndev) for d in range(1, ndev)]
-    joined = _greet([_at(p // nseq, lax.rem(p, nseq)) for p in far])
+    core, chip = lax.rem(me, 2), me // 2
+
+    def spot(p):
+        return _at(p // nseq, lax.rem(p, nseq))
+
+    far = [_flip(me, d) for d in range(ndev - 1, 0, -1)]
+    joined = _greet([spot(p) for p in far])
     eye = (lax.broadcasted_iota(jnp.int32, (batch, hd), 0)
            == lax.broadcasted_iota(jnp.int32, (batch, hd), 1))
-    y = None
+    attn = []
     for e in range(per):
         line = per * batch + 2 * e
         tops = [got[i][line:line + 1, :] for i in range(nseq)]
@@ -244,36 +262,50 @@
             term = got[i][e * batch:(e + 1) * batch, :] * down
             mix = term if mix is None else mix + term
         down = jnp.sum(jnp.where(eye, total, 0.0), axis=1, keepdims=True)
-        attn = (mix / down).astype(BF16)
-        term = jnp.dot(attn, wo[e * hd:(e + 1) * hd, :], preferred_element_type=F32)
-        y = term if y is None else y + term
-    for p in range(ndev):
-        ysend[p] = y[:, p * cols:(p + 1) * cols]
+        attn.append((mix / down).astype(BF16))
+    attn = jnp.concatenate(attn, axis=-1)
+
+    def product(j, side):
+        at = pl.multiple_of((2 * j + side) * cols, 128)
+        return jnp.dot(attn, wo[:, pl.ds(at, cols)], preferred_element_type=F32)
+
+    for j in range(chips):
+        theirs[j] = product(j, 1 - core)
     joined()
+    swap = pltpu.make_async_remote_copy(
+        src_ref=theirs, dst_ref=half, send_sem=s1, recv_sem=r1,
+        device_id=spot(_flip(me, 1)), device_id_type=MESH)
+    swap.start()
+    for j in range(chips):
+        ours[j] = product(j, core)
+    swap.wait_recv()
+    for j in range(chips):
+        ours[j] += half[j]
     moves = []
-    for i, p in enumerate(far):
+    for i in range(chips - 1):
+        there = _flip(chip, chips - 1 - i)
         c = pltpu.make_async_remote_copy(
-            src_ref=ysend.at[p], dst_ref=ygot.at[i], send_sem=s2.at[i], recv_sem=r2.at[i],
-            device_id=_at(p // nseq, lax.rem(p, nseq)), device_id_type=MESH)
+            src_ref=ours.at[there], dst_ref=ygot.at[i], send_sem=s2.at[i], recv_sem=r2.at[i],
+            device_id=spot(2 * there + core), device_id_type=MESH)
         c.start()
         moves.append(c)
-    acc = ysend[me]
-    for i, c in enumerate(moves):
-        c.wait_recv()
+    acc = ours[chip]
+    for i in range(chips - 2, -1, -1):
+        moves[i].wait_recv()
         acc = acc + ygot[i]
     yout[me] = acc.astype(BF16)
     shares = []
     for i, p in enumerate(far):
         c = pltpu.make_async_remote_copy(
             src_ref=yout.at[me], dst_ref=yout.at[me], send_sem=s3.at[i], recv_sem=r3.at[i],
-            device_id=_at(p // nseq, lax.rem(p, nseq)), device_id_type=MESH)
+            device_id=spot(p), device_id_type=MESH)
         c.start()
         shares.append(c)
     for c in shares:
         c.wait_recv()
     for p in range(ndev):
         y_ref[:, p * cols:(p + 1) * cols] = yout[p]
-    for c in moves + shares:
+    for c in [swap] + moves + shares:
         c.wait_send()
 
 
@@ -297,17 +329,17 @@
         qkv, kring, vring = pl.pallas_call(
             project_kernel,
             out_shape=(jax.ShapeDtypeStruct((3, 2, batch * heads, 128), F32), ring, ring),
-            in_specs=[pl.BlockSpec(memory_space=pltpu.HBM)] + [any_spec] * 5,
+            in_specs=[any_spec] * 6,
             out_specs=(vmem, vmem, vmem),
             scratch_shapes=[
                 pltpu.VMEM(tokens.shape, BF16),
                 pltpu.VMEM((3, PARTS, model // PARTS, cols), BF16),
                 pltpu.VMEM((nseq, 3, batch, cols), BF16),
-                dma, dma((3, PARTS)), dma((2, AHEAD)), dma((3, nseq - 1)), dma((3, nseq - 1)),
+                dma, dma((3, PARTS)), dma((2, HELD)), dma((3, nseq - 1)), dma((3, nseq - 1)),
             ],
             compiler_params=pltpu.CompilerParams(
                 collective_id=0, has_side_effects=True, vmem_limit_bytes=11 * 2**20),
-        )(tokens, w_query, w_key, w_value, k_flat, v_flat)
+        )(pltpu.with_memory_space_constraint(tokens, pltpu.HBM), w_query, w_key, w_value, k_flat, v_flat)
         chunk = jax.ShapeDtypeStruct((per * batch + 8, hd), F32)
         chunk = jax.ShapeDtypeStruct((per * batch + 8, hd), F32)
         k_out, v_out, kring, vring, *chunks = pl.pallas_call(
@@ -342,10 +374,12 @@
             in_specs=[vmem] * (nseq + 2),
             out_specs=vmem,
             scratch_shapes=[
-                pltpu.VMEM((ndev, batch, ycols), F32),
-                pltpu.VMEM((ndev, batch, ycols), F32),
+                pltpu.VMEM((ndev // 2, batch, ycols), F32),
+                pltpu.VMEM((ndev // 2, batch, ycols), F32),
+                pltpu.VMEM((ndev // 2, batch, ycols), F32),
+                pltpu.VMEM((ndev // 2 - 1, batch, ycols), F32),
                 pltpu.VMEM((ndev, batch, ycols), BF16),
-                dma((ndev,)), dma((ndev,)), dma((ndev,)), dma((ndev,)),
+                dma, dma, dma((ndev // 2 - 1,)), dma((ndev // 2 - 1,)), dma((ndev - 1,)), dma((ndev - 1,)),
             ],
             compiler_params=pltpu.CompilerParams(
                 collective_id=1, has_side_effects=True, vmem_limit_bytes=6 * 2**20),

time: 69.3 us -> 68.5 us (0.988)
  local copies, waits for them, and re-layouts: 1.61 us -> 0.69 us
    pallas_call x1, Pallas kernels: 10.8 us -> 12.6 us  [local_step(): pl.pallas_call(project_kernel, out_shape=(jax.ShapeDtypeStruct((3, 2, bat...]
    pallas_call x1, Pallas kernels: 13 us -> 11.7 us  [local_step(): pl.pallas_call(finish_kernel, out_shape=jax.ShapeDtypeStruct((batch, mode...]
    unnamed x7 -> x5, local copies, waits for them, and re-layouts: 1.61 us -> 0.69 us
where the time goes in v1:
time: 68.5 us; the launch traced here: 68.4 us
  Pallas kernels  65.2 us (95%)
  starting transfers between devices  1.88 us (3%)
  between operations  0.71 us (1%)
  local copies, waits for them, and re-layouts  0.69 us (1%)
    pallas_call x1, Pallas kernels, local_step(): pl.pallas_call(functools.partial(attend_kernel, hd ** (-0.5)), out_shape=...  34.5 us
    pallas_call x1, Pallas kernels, local_step(): pl.pallas_call(project_kernel, out_shape=(jax.ShapeDtypeStruct((3, 2, bat...  12.6 us
    pallas_call x1, Pallas kernels, local_step(): pl.pallas_call(finish_kernel, out_shape=jax.ShapeDtypeStruct((batch, mode...  11.7 us
    pallas_call x1, Pallas kernels, local_step(): pl.pallas_call(write_kernel, out_shape=(cache, cache, jax.ShapeDtypeStruc...  6.39 us
    ppermute x3, starting transfers between devices, local_step(): lax.ppermute(chunks[d], 'seq', [(i, i ^ d) for i in range(nseq)])  1.88 us
  transfers between devices with their start and end apart: 3, of which 0 were waited for; matrix products, arithmetic and copies ran while one was open for 0% of the time, Pallas kernels for 9%

profile of v1, /device:TPU:0, one launch (start us, length us, event | category | flops | bytes accessed | tf_op | source)
XLA Modules:
  0.0 68.4 jit_solution(843815394453240132)
XLA Ops:
  0.6 0.0 copy-start.1
  0.6 12.6 %shard_map.103 = (f32[3,2,256,128]{3,2,1,0:T(8,128)S(1)}, bf16[16,2048,256]{2,1,0:T(8,128)(2,1)S(1)}, bf16[16,2048,256]{2,1,0:T(8,128)(2,1)S(1)}) custom-call(bf16[32,3072]{1,0:T(8,128)(2,1)} %x_hbm.1, bf16[3072,4096]{1,0:T(8,128)(2,1)} %wq_ref.1, bf16[3072,4096]{1,0:T(8,128)(2,1)} %wk_ref.1, bf16[3072,4096]{1,0:T(8,128)(2,1)} %wv_ref.1, ...), custom_call_target="tpu_custom_call" | custom-call | tf_op jit(solution)/shard_map/pallas_call | solution.py:329
  13.2 0.0 copy-done.1
  13.2 34.5 %shard_map.104 = (bf16[32,2048,256]{2,1,0:T(8,128)(2,1)}, bf16[32,2048,256]{2,1,0:T(8,128)(2,1)}, bf16[16,2048,256]{2,1,0:T(8,128)(2,1)S(1)}, bf16[16,2048,256]{...) custom-call(s32[32]{0:T(128)S(1)} %copy-done.1, ...), custom_call_target="tpu_custom_call", output_to_operand_aliasing={{2}: (4, {}), {3}: (5, {})} | custom-call | tf_op jit(solution)/shard_map/pallas_call | solution.py:345
  47.7 0.2 collective-permute-start
  47.9 0.6 collective-permute-start.1
  48.5 1.1 %collective-permute-start.2 = (f32[72,256]{1,0:T(8,128)S(1)}, f32[72,256]{1,0:T(8,128)S(1)}, u32[]{:S(2)}, u32[]{:S(2)}) collective-permute-start(f32[72,256]{1,0:T(8,128)S(1)} %get-tuple-element.23), channel_id=1, source_target_pairs={{0,3},{1,2},{2,1},{3,0},{4,7},{5,6},{6,5},{7,4}} | collective-permute-start | bytes 221192 | tf_op jit(solution)/shard_map/ppermute | solution.py:359
  49.6 0.0 copy-start
  49.6 6.4 %shard_map.105 = (bf16[32,2048,256]{2,1,0:T(8,128)(2,1)}, bf16[32,2048,256]{2,1,0:T(8,128)(2,1)}, f32[8,128]{1,0:T(8,128)S(1)}) custom-call(bf16[16,2048,256]{2,1,0:T(8,128)(2,1)S(1)} %get-tuple-element.24.kring, bf16[16,2048,256]{2,1,0:T(8,128)(2,1)S(1)} %get-tuple-element.25.vring, ...), custom_call_target="tpu_custom_call", output_to_operand_aliasing={{0}: (2, {}), {1}: (3, {})} | custom-call | flops 1000000000 | bytes 33554432 | tf_op jit(solution)/shard_map/pallas_call | solution.py:360
  56.0 0.0 collective-permute-done.refs_1_
  56.0 0.0 collective-permute-done.1.refs_2_
  56.0 0.0 collective-permute-done.2.refs_3_
  56.1 0.0 copy-done
  56.1 11.7 %shard_map.106 = bf16[32,3072]{1,0:T(8,128)(2,1)S(1)} custom-call(f32[72,256]{1,0:T(8,128)S(1)} %get-tuple-element.20.chunk.refs_0_, f32[72,256]{1,0:T(8,128)S(1)} %collective-permute-done.refs_1_, f32[72,256]{1,0:T(8,128)S(1)} %collective-permute-done.1.refs_2_, f32[72,256]{1,0:T(8,128)S(1)} %collective-permute-done.2.refs_3_, ...), custom_call_target="tpu_custom_call" | custom-call | tf_op jit(solution)/shard_map/pallas_call | solution.py:371
  67.8 0.7 copy.20
Async XLA Ops:
  0.6 12.6 %copy-start.1 = (s32[32]{0:T(128)S(1)}, s32[32]{0:T(128)}, u32[]{:S(2)}) copy-start(s32[32]{0:T(128)} %pos_ref.1) | copy-start | bytes 388
  47.7 8.3 %collective-permute-start = (f32[72,256]{1,0:T(8,128)S(1)}, f32[72,256]{1,0:T(8,128)S(1)}, u32[]{:S(2)}, u32[]{:S(2)}) collective-permute-start(f32[72,256]{1,0:T(8,128)S(1)} %get-tuple-element.21), channel_id=1, source_target_pairs={{0,1},{1,0},{2,3},{3,2},{4,5},{5,4},{6,7},{7,6}} | collective-permute-start | bytes 221192 | tf_op jit(solution)/shard_map/ppermute | solution.py:359
  47.9 8.1 %collective-permute-start.1 = (f32[72,256]{1,0:T(8,128)S(1)}, f32[72,256]{1,0:T(8,128)S(1)}, u32[]{:S(2)}, u32[]{:S(2)}) collective-permute-start(f32[72,256]{1,0:T(8,128)S(1)} %get-tuple-element.22), channel_id=1, source_target_pairs={{0,2},{1,3},{2,0},{3,1},{4,6},{5,7},{6,4},{7,5}} | collective-permute-start | bytes 221192 | tf_op jit(solution)/shard_map/ppermute | solution.py:359
  48.5 7.5 %collective-permute-start.2 = (f32[72,256]{1,0:T(8,128)S(1)}, f32[72,256]{1,0:T(8,128)S(1)}, u32[]{:S(2)}, u32[]{:S(2)}) collective-permute-start(f32[72,256]{1,0:T(8,128)S(1)} %get-tuple-element.23), channel_id=1, source_target_pairs={{0,3},{1,2},{2,1},{3,0},{4,7},{5,6},{6,5},{7,4}} | collective-permute-start | bytes 221192 | tf_op jit(solution)/shard_map/ppermute | solution.py:359
  49.6 6.4 %copy-start = (bf16[512,3072]{1,0:T(8,128)(2,1)S(1)}, bf16[512,3072]{1,0:T(8,128)(2,1)}, u32[]{:S(2)}) copy-start(bf16[512,3072]{1,0:T(8,128)(2,1)} %refs_4_.1) | copy-start | bytes 9437188

commit v2 on v1

--- a/solution.py
+++ b/solution.py
@@ -9,8 +9,10 @@
 
 MESH = pl.DeviceIdType.MESH
 RING = 8
-HELD = 4
-AHEAD = 2
+HELD = 3
+FIRST = 4
+AHEAD = 3
+LATE = 5
 PARTS = 4
 F32 = jnp.float32
 BF16 = jnp.bfloat16
@@ -55,7 +57,7 @@
             c.start()
             loads.append(c)
     ring = []
-    for b in range(HELD):
+    for b in range(FIRST):
         for i, (src, dst) in enumerate(((k_hbm, kring), (v_hbm, vring))):
             pair = pl.ds(2 * b, 2)
             ring.append(pltpu.make_async_copy(src.at[pair], dst.at[pair], ringsem.at[i, b]))
@@ -66,7 +68,7 @@
         acc = None
         for p in range(PARTS):
             loads[j * PARTS + p].wait()
-            share = -(-len(ring) * (j * PARTS + p + 1) // (3 * PARTS))
+            share = len(ring) * (j * PARTS + p + 1 - LATE) // (3 * PARTS - LATE)
             while asked < share:
                 ring[asked].start()
                 asked += 1
@@ -138,21 +140,24 @@
     def fresh(j, lines):
         return jnp.concatenate([qkv_ref[j, 0, lines, :], qkv_ref[j, 1, lines, :]], axis=-1).astype(BF16)
 
-    for i in range(HELD, HELD + flow):
+    for i in range(FIRST, FIRST + 2):
         for c in reads(i):
             c.start()
 
     def body(i, carry):
         nxt = i + AHEAD
 
-        @pl.when(jnp.logical_and(nxt >= RING, nxt < pairs))
+        @pl.when(jnp.logical_and(nxt >= FIRST + 2, nxt < pairs))
         def _():
-            for c in writes(nxt - flow):
-                c.wait()
+            @pl.when(nxt >= RING)
+            def _():
+                for c in writes(nxt - flow):
+                    c.wait()
+
             for c in reads(nxt):
                 c.start()
 
-        @pl.when(i >= HELD)
+        @pl.when(i >= FIRST)
         def _():
             for c in reads(i):
                 c.wait()
@@ -187,7 +192,7 @@
             mbuf[lines, :] = jnp.broadcast_to(top, (heads, 128))
             lbuf[lines, :] = jnp.broadcast_to(total, (heads, 128))
 
-        @pl.when(i >= HELD)
+        @pl.when(jnp.logical_and(i >= HELD, i < pairs - 1))
         def _():
             for c in writes(i):
                 c.start()
@@ -210,17 +215,19 @@
                 chunk[line:line + 1, 128:] = jnp.zeros((1, hd - 128), F32)
         used = per * batch + 2 * per
         chunk[used:, :] = jnp.zeros((chunk.shape[0] - used, hd), F32)
-    for i in range(pairs - flow, pairs):
+    for i in range(pairs - flow, pairs - 1):
         for c in writes(i):
             c.wait()
 
 
 def write_kernel(kring, vring, ko_in, vo_in, chunk, ko_hbm, vo_hbm, done, sem):
+    pairs = ko_hbm.shape[0] // 2
+    last = HELD + (pairs - 1 - HELD) % (RING - HELD)
     copies = []
-    for i in range(HELD):
+    for i, slot in [(i, i) for i in range(HELD)] + [(pairs - 1, last)]:
         for src, dst in ((kring, ko_hbm), (vring, vo_hbm)):
-            pair = pl.ds(i * 2, 2)
-            c = pltpu.make_async_copy(src.at[pair], dst.at[pair], sem.at[len(copies)])
+            c = pltpu.make_async_copy(
+                src.at[pl.ds(slot * 2, 2)], dst.at[pl.ds(i * 2, 2)], sem.at[len(copies)])
             c.start()
             copies.append(c)
     done[...] = jnp.zeros_like(done)
@@ -335,7 +342,7 @@
                 pltpu.VMEM(tokens.shape, BF16),
                 pltpu.VMEM((3, PARTS, model // PARTS, cols), BF16),
                 pltpu.VMEM((nseq, 3, batch, cols), BF16),
-                dma, dma((3, PARTS)), dma((2, HELD)), dma((3, nseq - 1)), dma((3, nseq - 1)),
+                dma, dma((3, PARTS)), dma((2, FIRST)), dma((3, nseq - 1)), dma((3, nseq - 1)),
             ],
             compiler_params=pltpu.CompilerParams(
                 collective_id=0, has_side_effects=True, vmem_limit_bytes=11 * 2**20),
@@ -363,9 +370,9 @@
             in_specs=[vmem, vmem, any_spec, any_spec, vmem],
             out_specs=(any_spec, any_spec, vmem),
             input_output_aliases={2: 0, 3: 1},
-            scratch_shapes=[dma((2 * HELD,))],
+            scratch_shapes=[dma((2 * HELD + 2,))],
             compiler_params=pltpu.CompilerParams(vmem_limit_bytes=1 * 2**20),
-            cost_estimate=pl.CostEstimate(flops=10**9, bytes_accessed=8 * HELD * 2**20, transcendentals=0),
+            cost_estimate=pl.CostEstimate(flops=10**9, bytes_accessed=2**24, transcendentals=0),
         )(kring, vring, k_out, v_out, chunks[0])
         ycols = model // ndev
         y = pl.pallas_call(

time: 68.5 us -> 69.7 us (1.018)
  Pallas kernels: 65.2 us -> 66.6 us
    pallas_call x1, Pallas kernels: 34.5 us -> 35.5 us  [local_step(): pl.pallas_call(functools.partial(attend_kernel, hd ** (-0.5)), out_shape=...]
where the time goes in v2:
time: 69.7 us; the launch traced here: 70 us
  Pallas kernels  66.6 us (96%)
  starting transfers between devices  2.03 us (3%)
  between operations  0.71 us (1%)
    pallas_call x1, Pallas kernels, local_step(): pl.pallas_call(functools.partial(attend_kernel, hd ** (-0.5)), out_shape=...  35.5 us
    pallas_call x1, Pallas kernels, local_step(): pl.pallas_call(project_kernel, out_shape=(jax.ShapeDtypeStruct((3, 2, bat...  12.6 us
    pallas_call x1, Pallas kernels, local_step(): pl.pallas_call(finish_kernel, out_shape=jax.ShapeDtypeStruct((batch, mode...  12.1 us
    pallas_call x1, Pallas kernels, local_step(): pl.pallas_call(write_kernel, out_shape=(cache, cache, jax.ShapeDtypeStruc...  6.39 us
    ppermute x3, starting transfers between devices, local_step(): lax.ppermute(chunks[d], 'seq', [(i, i ^ d) for i in range(nseq)])  2.03 us
  transfers between devices with their start and end apart: 3, of which 0 were waited for; matrix products, arithmetic and copies ran while one was open for 0% of the time, Pallas kernels for 9%

profile of v2, /device:TPU:0, one launch (start us, length us, event | category | flops | bytes accessed | tf_op | source)
XLA Modules:
  0.0 70.0 jit_solution(14584085255832517829)
XLA Ops:
  0.6 0.0 copy-start.1
  0.6 12.6 %shard_map.103 = (f32[3,2,256,128]{3,2,1,0:T(8,128)S(1)}, bf16[16,2048,256]{2,1,0:T(8,128)(2,1)S(1)}, bf16[16,2048,256]{2,1,0:T(8,128)(2,1)S(1)}) custom-call(bf16[32,3072]{1,0:T(8,128)(2,1)} %x_hbm.1, bf16[3072,4096]{1,0:T(8,128)(2,1)} %wq_ref.1, bf16[3072,4096]{1,0:T(8,128)(2,1)} %wk_ref.1, bf16[3072,4096]{1,0:T(8,128)(2,1)} %wv_ref.1, ...), custom_call_target="tpu_custom_call" | custom-call | tf_op jit(solution)/shard_map/pallas_call | solution.py:336
  13.2 0.0 copy-done.1
  13.2 35.5 %shard_map.104 = (bf16[32,2048,256]{2,1,0:T(8,128)(2,1)}, bf16[32,2048,256]{2,1,0:T(8,128)(2,1)}, bf16[16,2048,256]{2,1,0:T(8,128)(2,1)S(1)}, bf16[16,2048,256]{...) custom-call(s32[32]{0:T(128)S(1)} %copy-done.1, ...), custom_call_target="tpu_custom_call", output_to_operand_aliasing={{2}: (4, {}), {3}: (5, {})} | custom-call | tf_op jit(solution)/shard_map/pallas_call | solution.py:352
  48.7 0.1 collective-permute-start
  48.9 1.8 %collective-permute-start.1 = (f32[72,256]{1,0:T(8,128)S(1)}, f32[72,256]{1,0:T(8,128)S(1)}, u32[]{:S(2)}, u32[]{:S(2)}) collective-permute-start(f32[72,256]{1,0:T(8,128)S(1)} %get-tuple-element.22), channel_id=1, source_target_pairs={{0,2},{1,3},{2,0},{3,1},{4,6},{5,7},{6,4},{7,5}} | collective-permute-start | bytes 221192 | tf_op jit(solution)/shard_map/ppermute | solution.py:366
  50.7 0.1 collective-permute-start.2
  50.8 0.0 copy-start
  50.8 6.4 %shard_map.105 = (bf16[32,2048,256]{2,1,0:T(8,128)(2,1)}, bf16[32,2048,256]{2,1,0:T(8,128)(2,1)}, f32[8,128]{1,0:T(8,128)S(1)}) custom-call(bf16[16,2048,256]{2,1,0:T(8,128)(2,1)S(1)} %get-tuple-element.24.kring, bf16[16,2048,256]{2,1,0:T(8,128)(2,1)S(1)} %get-tuple-element.25.vring, ...), custom_call_target="tpu_custom_call", output_to_operand_aliasing={{0}: (2, {}), {1}: (3, {})} | custom-call | flops 1000000000 | bytes 16777216 | tf_op jit(solution)/shard_map/pallas_call | solution.py:367
  57.2 0.0 collective-permute-done.refs_1_
  57.2 0.0 collective-permute-done.1.refs_2_
  57.2 0.0 collective-permute-done.2.refs_3_
  57.2 0.0 copy-done
  57.2 12.1 %shard_map.106 = bf16[32,3072]{1,0:T(8,128)(2,1)S(1)} custom-call(f32[72,256]{1,0:T(8,128)S(1)} %get-tuple-element.20.chunk.refs_0_, f32[72,256]{1,0:T(8,128)S(1)} %collective-permute-done.refs_1_, f32[72,256]{1,0:T(8,128)S(1)} %collective-permute-done.1.refs_2_, f32[72,256]{1,0:T(8,128)S(1)} %collective-permute-done.2.refs_3_, ...), custom_call_target="tpu_custom_call" | custom-call | tf_op jit(solution)/shard_map/pallas_call | solution.py:378
  69.3 0.7 copy.20
Async XLA Ops:
  0.6 12.6 %copy-start.1 = (s32[32]{0:T(128)S(1)}, s32[32]{0:T(128)}, u32[]{:S(2)}) copy-start(s32[32]{0:T(128)} %pos_ref.1) | copy-start | bytes 388
  48.7 8.4 %collective-permute-start = (f32[72,256]{1,0:T(8,128)S(1)}, f32[72,256]{1,0:T(8,128)S(1)}, u32[]{:S(2)}, u32[]{:S(2)}) collective-permute-start(f32[72,256]{1,0:T(8,128)S(1)} %get-tuple-element.21), channel_id=1, source_target_pairs={{0,1},{1,0},{2,3},{3,2},{4,5},{5,4},{6,7},{7,6}} | collective-permute-start | bytes 221192 | tf_op jit(solution)/shard_map/ppermute | solution.py:366
  48.9 8.3 %collective-permute-start.1 = (f32[72,256]{1,0:T(8,128)S(1)}, f32[72,256]{1,0:T(8,128)S(1)}, u32[]{:S(2)}, u32[]{:S(2)}) collective-permute-start(f32[72,256]{1,0:T(8,128)S(1)} %get-tuple-element.22), channel_id=1, source_target_pairs={{0,2},{1,3},{2,0},{3,1},{4,6},{5,7},{6,4},{7,5}} | collective-permute-start | bytes 221192 | tf_op jit(solution)/shard_map/ppermute | solution.py:366
  50.7 6.5 %collective-permute-start.2 = (f32[72,256]{1,0:T(8,128)S(1)}, f32[72,256]{1,0:T(8,128)S(1)}, u32[]{:S(2)}, u32[]{:S(2)}) collective-permute-start(f32[72,256]{1,0:T(8,128)S(1)} %get-tuple-element.23), channel_id=1, source_target_pairs={{0,3},{1,2},{2,1},{3,0},{4,7},{5,6},{6,5},{7,4}} | collective-permute-start | bytes 221192 | tf_op jit(solution)/shard_map/ppermute | solution.py:366
  50.8 6.4 %copy-start = (bf16[512,3072]{1,0:T(8,128)(2,1)S(1)}, bf16[512,3072]{1,0:T(8,128)(2,1)}, u32[]{:S(2)}) copy-start(bf16[512,3072]{1,0:T(8,128)(2,1)} %refs_4_.1) | copy-start | bytes 9437188

commit v3 on v2

--- a/solution.py
+++ b/solution.py
@@ -8,12 +8,11 @@
 from jax.sharding import PartitionSpec as P
 
 MESH = pl.DeviceIdType.MESH
-RING = 8
-HELD = 3
+BURST = 4
+RING = 2 * BURST
 FIRST = 4
-AHEAD = 3
-LATE = 5
-PARTS = 4
+EARLY = 3
+PARTS = 1
 F32 = jnp.float32
 BF16 = jnp.bfloat16
 NT = (((1,), (1,)), ((), ()))
@@ -68,7 +67,7 @@
         acc = None
         for p in range(PARTS):
             loads[j * PARTS + p].wait()
-            share = len(ring) * (j * PARTS + p + 1 - LATE) // (3 * PARTS - LATE)
+            share = -(-len(ring) * (j * PARTS + p + 1) // (3 * PARTS))
             while asked < share:
                 ring[asked].start()
                 asked += 1
@@ -122,42 +121,43 @@
     def both(i):
         return pl.ds(pl.multiple_of(i * 2, 2), 2)
 
-    flow = RING - HELD
-
-    def place(i):
-        return HELD + lax.rem(i - HELD, flow)
-
     def reads(i):
-        slot = place(i)
+        slot = lax.rem(i, RING)
         return [pltpu.make_async_copy(src.at[both(i)], dst.at[both(slot)], sem.at[slot])
                 for src, dst, sem in ((k_hbm, kring, kin), (v_hbm, vring, vin))]
 
     def writes(i):
-        slot = place(i)
-        return [pltpu.make_async_copy(src.at[both(slot)], dst.at[both(i)], sem.at[slot])
-                for src, dst, sem in ((kring, ko_hbm, kout), (vring, vo_hbm, vout))]
+        slot = lax.rem(i, RING)
+        return [pltpu.make_async_copy(src.at[2 * slot + g], dst.at[2 * i + g], sem.at[2 * slot + g])
+                for g in range(2) for src, dst, sem in ((kring, ko_hbm, kout), (vring, vo_hbm, vout))]
 
     def fresh(j, lines):
         return jnp.concatenate([qkv_ref[j, 0, lines, :], qkv_ref[j, 1, lines, :]], axis=-1).astype(BF16)
 
-    for i in range(FIRST, FIRST + 2):
+    for i in range(FIRST, RING):
         for c in reads(i):
             c.start()
 
     def body(i, carry):
-        nxt = i + AHEAD
-
-        @pl.when(jnp.logical_and(nxt >= FIRST + 2, nxt < pairs))
+        step = lax.rem(i, BURST)
+        slot = lax.rem(i, RING)
+
+        @pl.when(jnp.logical_and(step == 0, i > 0))
         def _():
-            @pl.when(nxt >= RING)
-            def _():
-                for c in writes(nxt - flow):
-                    c.wait()
-
-            for c in reads(nxt):
-                c.start()
-
-        @pl.when(i >= FIRST)
+            for g in range(EARLY):
+                if g < FIRST - BURST:
+                    @pl.when(i > BURST)
+                    def _():
+                        for c in reads(i + g):
+                            c.wait()
+                else:
+                    for c in reads(i + g):
+                        c.wait()
+            for g in range(BURST):
+                for c in writes(i - BURST + g):
+                    c.start()
+
+        @pl.when(jnp.logical_and(step >= EARLY, i >= FIRST))
         def _():
             for c in reads(i):
                 c.wait()
@@ -169,7 +169,7 @@
             at = pos - base
             lines = pl.ds(pl.multiple_of(b * heads, heads), heads)
             spot = pl.ds(pl.multiple_of(at * heads, heads), heads)
-            ks = 2 * jnp.where(i < HELD, i, place(jnp.maximum(i, HELD))) + g
+            ks = 2 * slot + g
 
             @pl.when(jnp.logical_and(at >= 0, at < span))
             def _():
@@ -192,10 +192,13 @@
             mbuf[lines, :] = jnp.broadcast_to(top, (heads, 128))
             lbuf[lines, :] = jnp.broadcast_to(total, (heads, 128))
 
-        @pl.when(jnp.logical_and(i >= HELD, i < pairs - 1))
+        @pl.when(jnp.logical_and(step == BURST - 1, jnp.logical_and(i > BURST, i < pairs - 1)))
         def _():
-            for c in writes(i):
-                c.start()
+            for g in range(BURST):
+                for c in writes(i + 1 - 2 * BURST + g):
+                    c.wait()
+                for c in reads(i + 1 + g):
+                    c.start()
 
         return carry
 
@@ -215,19 +218,18 @@
                 chunk[line:line + 1, 128:] = jnp.zeros((1, hd - 128), F32)
         used = per * batch + 2 * per
         chunk[used:, :] = jnp.zeros((chunk.shape[0] - used, hd), F32)
-    for i in range(pairs - flow, pairs - 1):
+    for i in range(pairs - 2 * BURST, pairs - BURST):
         for c in writes(i):
             c.wait()
 
 
 def write_kernel(kring, vring, ko_in, vo_in, chunk, ko_hbm, vo_hbm, done, sem):
     pairs = ko_hbm.shape[0] // 2
-    last = HELD + (pairs - 1 - HELD) % (RING - HELD)
     copies = []
-    for i, slot in [(i, i) for i in range(HELD)] + [(pairs - 1, last)]:
+    for i in range(pairs - BURST, pairs):
         for src, dst in ((kring, ko_hbm), (vring, vo_hbm)):
             c = pltpu.make_async_copy(
-                src.at[pl.ds(slot * 2, 2)], dst.at[pl.ds(i * 2, 2)], sem.at[len(copies)])
+                src.at[pl.ds(i % RING * 2, 2)], dst.at[pl.ds(i * 2, 2)], sem.at[len(copies)])
             c.start()
             copies.append(c)
     done[...] = jnp.zeros_like(done)
@@ -359,7 +361,7 @@
                 pltpu.VMEM((2, batch * heads, 128), F32),
                 pltpu.VMEM((batch * heads, 128), F32),
                 pltpu.VMEM((batch * heads, 128), F32),
-                dma((RING,)), dma((RING,)), dma((RING,)), dma((RING,)),
+                dma((2 * RING,)), dma((2 * RING,)), dma((2 * RING,)), dma((2 * RING,)),
             ],
             compiler_params=pltpu.CompilerParams(vmem_limit_bytes=4 * 2**20),
         )(positions, qkv, k_flat, v_flat, kring, vring)
@@ -370,7 +372,7 @@
             in_specs=[vmem, vmem, any_spec, any_spec, vmem],
             out_specs=(any_spec, any_spec, vmem),
             input_output_aliases={2: 0, 3: 1},
-            scratch_shapes=[dma((2 * HELD + 2,))],
+            scratch_shapes=[dma((2 * BURST,))],
             compiler_params=pltpu.CompilerParams(vmem_limit_bytes=1 * 2**20),
             cost_estimate=pl.CostEstimate(flops=10**9, bytes_accessed=2**24, transcendentals=0),
         )(kring, vring, k_out, v_out, chunks[0])

time: 69.7 us -> 65 us (0.933)
  Pallas kernels: 66.6 us -> 61.6 us
    pallas_call x1, Pallas kernels: 35.5 us -> 31.9 us  [local_step(): pl.pallas_call(functools.partial(attend_kernel, hd ** (-0.5)), out_shape=...]
    pallas_call x1, Pallas kernels: 12.6 us -> 11.7 us  [local_step(): pl.pallas_call(project_kernel, out_shape=(jax.ShapeDtypeStruct((3, 2, bat...]
  transfers between devices with their start and end apart: 3 -> 3, of which waited for: 0 -> 0; matrix products, arithmetic and copies ran while one was open for 0% -> 0% of each run, Pallas kernels for 9% -> 10%
where the time goes in v3:
time: 65 us; the launch traced here: 64.9 us
  Pallas kernels  61.6 us (95%)
  starting transfers between devices  1.88 us (3%)
  between operations  0.71 us (1%)
  local copies, waits for them, and re-layouts  0.69 us (1%)
    pallas_call x1, Pallas kernels, local_step(): pl.pallas_call(functools.partial(attend_kernel, hd ** (-0.5)), out_shape=...  31.9 us
    pallas_call x1, Pallas kernels, local_step(): pl.pallas_call(project_kernel, out_shape=(jax.ShapeDtypeStruct((3, 2, bat...  11.7 us
    pallas_call x1, Pallas kernels, local_step(): pl.pallas_call(finish_kernel, out_shape=jax.ShapeDtypeStruct((batch, mode...  11.7 us
    pallas_call x1, Pallas kernels, local_step(): pl.pallas_call(write_kernel, out_shape=(cache, cache, jax.ShapeDtypeStruc...  6.39 us
    ppermute x3, starting transfers between devices, local_step(): lax.ppermute(chunks[d], 'seq', [(i, i ^ d) for i in range(nseq)])  1.88 us
  transfers between devices with their start and end apart: 3, of which 0 were waited for; matrix products, arithmetic and copies ran while one was open for 0% of the time, Pallas kernels for 10%

profile of v3, /device:TPU:0, one launch (start us, length us, event | category | flops | bytes accessed | tf_op | source)
XLA Modules:
  0.0 64.9 jit_solution(5983498277842574956)
XLA Ops:
  0.6 0.0 copy-start.1
  0.6 11.7 %shard_map.103 = (f32[3,2,256,128]{3,2,1,0:T(8,128)S(1)}, bf16[16,2048,256]{2,1,0:T(8,128)(2,1)S(1)}, bf16[16,2048,256]{2,1,0:T(8,128)(2,1)S(1)}) custom-call(bf16[32,3072]{1,0:T(8,128)(2,1)} %x_hbm.1, bf16[3072,4096]{1,0:T(8,128)(2,1)} %wq_ref.1, bf16[3072,4096]{1,0:T(8,128)(2,1)} %wk_ref.1, bf16[3072,4096]{1,0:T(8,128)(2,1)} %wv_ref.1, ...), custom_call_target="tpu_custom_call" | custom-call | tf_op jit(solution)/shard_map/pallas_call | solution.py:338
  12.3 0.0 copy-done.1
  12.3 31.9 %shard_map.104 = (bf16[32,2048,256]{2,1,0:T(8,128)(2,1)}, bf16[32,2048,256]{2,1,0:T(8,128)(2,1)}, bf16[16,2048,256]{2,1,0:T(8,128)(2,1)S(1)}, bf16[16,2048,256]{...) custom-call(s32[32]{0:T(128)S(1)} %copy-done.1, ...), custom_call_target="tpu_custom_call", output_to_operand_aliasing={{2}: (4, {}), {3}: (5, {})} | custom-call | tf_op jit(solution)/shard_map/pallas_call | solution.py:354
  44.2 0.2 collective-permute-start
  44.4 0.7 %collective-permute-start.1 = (f32[72,256]{1,0:T(8,128)S(1)}, f32[72,256]{1,0:T(8,128)S(1)}, u32[]{:S(2)}, u32[]{:S(2)}) collective-permute-start(f32[72,256]{1,0:T(8,128)S(1)} %get-tuple-element.22), channel_id=1, source_target_pairs={{0,2},{1,3},{2,0},{3,1},{4,6},{5,7},{6,4},{7,5}} | collective-permute-start | bytes 221192 | tf_op jit(solution)/shard_map/ppermute | solution.py:368
  45.1 1.0 %collective-permute-start.2 = (f32[72,256]{1,0:T(8,128)S(1)}, f32[72,256]{1,0:T(8,128)S(1)}, u32[]{:S(2)}, u32[]{:S(2)}) collective-permute-start(f32[72,256]{1,0:T(8,128)S(1)} %get-tuple-element.23), channel_id=1, source_target_pairs={{0,3},{1,2},{2,1},{3,0},{4,7},{5,6},{6,5},{7,4}} | collective-permute-start | bytes 221192 | tf_op jit(solution)/shard_map/ppermute | solution.py:368
  46.1 0.0 copy-start
  46.1 6.4 %shard_map.105 = (bf16[32,2048,256]{2,1,0:T(8,128)(2,1)}, bf16[32,2048,256]{2,1,0:T(8,128)(2,1)}, f32[8,128]{1,0:T(8,128)S(1)}) custom-call(bf16[16,2048,256]{2,1,0:T(8,128)(2,1)S(1)} %get-tuple-element.24.kring, bf16[16,2048,256]{2,1,0:T(8,128)(2,1)S(1)} %get-tuple-element.25.vring, ...), custom_call_target="tpu_custom_call", output_to_operand_aliasing={{0}: (2, {}), {1}: (3, {})} | custom-call | flops 1000000000 | bytes 16777216 | tf_op jit(solution)/shard_map/pallas_call | solution.py:369
  52.5 0.0 collective-permute-done.refs_1_
  52.5 0.0 collective-permute-done.1.refs_2_
  52.5 0.0 collective-permute-done.2.refs_3_
  52.6 0.0 copy-done
  52.6 11.7 %shard_map.106 = bf16[32,3072]{1,0:T(8,128)(2,1)S(1)} custom-call(f32[72,256]{1,0:T(8,128)S(1)} %get-tuple-element.20.chunk.refs_0_, f32[72,256]{1,0:T(8,128)S(1)} %collective-permute-done.refs_1_, f32[72,256]{1,0:T(8,128)S(1)} %collective-permute-done.1.refs_2_, f32[72,256]{1,0:T(8,128)S(1)} %collective-permute-done.2.refs_3_, ...), custom_call_target="tpu_custom_call" | custom-call | tf_op jit(solution)/shard_map/pallas_call | solution.py:380
  64.2 0.7 %copy.20 = bf16[32,3072]{1,0:T(8,128)(2,1)} copy(bf16[32,3072]{1,0:T(8,128)(2,1)S(1)} %shard_map.106) | data formatting | bytes 393216
Async XLA Ops:
  0.6 11.7 %copy-start.1 = (s32[32]{0:T(128)S(1)}, s32[32]{0:T(128)}, u32[]{:S(2)}) copy-start(s32[32]{0:T(128)} %pos_ref.1) | copy-start | bytes 388
  44.2 8.3 %collective-permute-start = (f32[72,256]{1,0:T(8,128)S(1)}, f32[72,256]{1,0:T(8,128)S(1)}, u32[]{:S(2)}, u32[]{:S(2)}) collective-permute-start(f32[72,256]{1,0:T(8,128)S(1)} %get-tuple-element.21), channel_id=1, source_target_pairs={{0,1},{1,0},{2,3},{3,2},{4,5},{5,4},{6,7},{7,6}} | collective-permute-start | bytes 221192 | tf_op jit(solution)/shard_map/ppermute | solution.py:368
  44.4 8.1 %collective-permute-start.1 = (f32[72,256]{1,0:T(8,128)S(1)}, f32[72,256]{1,0:T(8,128)S(1)}, u32[]{:S(2)}, u32[]{:S(2)}) collective-permute-start(f32[72,256]{1,0:T(8,128)S(1)} %get-tuple-element.22), channel_id=1, source_target_pairs={{0,2},{1,3},{2,0},{3,1},{4,6},{5,7},{6,4},{7,5}} | collective-permute-start | bytes 221192 | tf_op jit(solution)/shard_map/ppermute | solution.py:368
  45.1 7.4 %collective-permute-start.2 = (f32[72,256]{1,0:T(8,128)S(1)}, f32[72,256]{1,0:T(8,128)S(1)}, u32[]{:S(2)}, u32[]{:S(2)}) collective-permute-start(f32[72,256]{1,0:T(8,128)S(1)} %get-tuple-element.23), channel_id=1, source_target_pairs={{0,3},{1,2},{2,1},{3,0},{4,7},{5,6},{6,5},{7,4}} | collective-permute-start | bytes 221192 | tf_op jit(solution)/shard_map/ppermute | solution.py:368
  46.1 6.4 %copy-start = (bf16[512,3072]{1,0:T(8,128)(2,1)S(1)}, bf16[512,3072]{1,0:T(8,128)(2,1)}, u32[]{:S(2)}) copy-start(bf16[512,3072]{1,0:T(8,128)(2,1)} %refs_4_.1) | copy-start | bytes 9437188

commit v4 on v2

--- a/solution.py
+++ b/solution.py
@@ -9,11 +9,28 @@
 
 MESH = pl.DeviceIdType.MESH
 RING = 8
-HELD = 3
+MORE = 2
 FIRST = 4
-AHEAD = 3
-LATE = 5
-PARTS = 4
+KEPT = 4
+SLOTS = (0, 1, 2, 3, 4, 5, 6, 7, 8, 9, 0, 1, 2, 3, 4, 5)
+
+
+def _plan(text):
+    return [(step[0], int(step[1:])) for step in text.split()]
+
+
+PLAN = (
+    _plan("r4 r5 r6 r7 a0 a1 a2 a3")
+    + _plan("R4 R5 R6 w0 w1 w2 w3")
+    + _plan("a4 a5 a6 R7 a7 r8 r9")
+    + _plan("W0 r10 W1 r11 W2 r12 W3 r13")
+    + _plan("R8 a8 R9 a9 R10 R11 R12")
+    + _plan("w4 w5 w6 w7 a10 w8 w9 a11")
+    + _plan("W4 r14 W5 r15 w10 w11 a12")
+    + _plan("R13 a13 R14 a14 R15 a15")
+    + _plan("W6 W7 W8 W9 W10 W11")
+)
+PARTS = 1
 F32 = jnp.float32
 BF16 = jnp.bfloat16
 NT = (((1,), (1,)), ((), ()))
@@ -68,7 +85,7 @@
         acc = None
         for p in range(PARTS):
             loads[j * PARTS + p].wait()
-            share = len(ring) * (j * PARTS + p + 1 - LATE) // (3 * PARTS - LATE)
+            share = -(-len(ring) * (j * PARTS + p + 1) // (3 * PARTS))
             while asked < share:
                 ring[asked].start()
                 asked += 1
@@ -105,8 +122,8 @@
 
 def attend_kernel(scale, pos_ref, qkv_ref, k_hbm, v_hbm, kring_in, vring_in,
                   ko_hbm, vo_hbm, kring, vring, *rest):
-    chunks = rest[:-7]
-    obuf, mbuf, lbuf, kin, vin, kout, vout = rest[-7:]
+    chunks = rest[:-9]
+    kmore, vmore, obuf, mbuf, lbuf, kin, vin, kout, vout = rest[-9:]
     batch, wide, hd = k_hbm.shape
     nseq = len(chunks)
     heads = obuf.shape[1] // batch
@@ -120,86 +137,76 @@
     slot_of = jnp.where(own, base + col // heads, batch * nseq * span)
 
     def both(i):
-        return pl.ds(pl.multiple_of(i * 2, 2), 2)
-
-    flow = RING - HELD
-
-    def place(i):
-        return HELD + lax.rem(i - HELD, flow)
+        return pl.ds(i * 2, 2)
+
+    def home(i):
+        slot = SLOTS[i]
+        return (kring, vring, slot, slot) if slot < RING else (kmore, vmore, slot - RING, slot)
 
     def reads(i):
-        slot = place(i)
-        return [pltpu.make_async_copy(src.at[both(i)], dst.at[both(slot)], sem.at[slot])
-                for src, dst, sem in ((k_hbm, kring, kin), (v_hbm, vring, vin))]
+        kbuf, vbuf, slot, sem = home(i)
+        return [pltpu.make_async_copy(src.at[both(i)], dst.at[both(slot)], done.at[sem])
+                for src, dst, done in ((k_hbm, kbuf, kin), (v_hbm, vbuf, vin))]
 
     def writes(i):
-        slot = place(i)
-        return [pltpu.make_async_copy(src.at[both(slot)], dst.at[both(i)], sem.at[slot])
-                for src, dst, sem in ((kring, ko_hbm, kout), (vring, vo_hbm, vout))]
+        kbuf, vbuf, slot, sem = home(i)
+        return [pltpu.make_async_copy(src.at[both(slot)], dst.at[both(i)], done.at[sem])
+                for src, dst, done in ((kbuf, ko_hbm, kout), (vbuf, vo_hbm, vout))]
 
     def fresh(j, lines):
         return jnp.concatenate([qkv_ref[j, 0, lines, :], qkv_ref[j, 1, lines, :]], axis=-1).astype(BF16)
 
-    for i in range(FIRST, FIRST + 2):
-        for c in reads(i):
+    def begin(copies):
+        for c in copies:
             c.start()
 
-    def body(i, carry):
-        nxt = i + AHEAD
-
-        @pl.when(jnp.logical_and(nxt >= FIRST + 2, nxt < pairs))
-        def _():
-            @pl.when(nxt >= RING)
-            def _():
-                for c in writes(nxt - flow):
-                    c.wait()
-
-            for c in reads(nxt):
-                c.start()
-
-        @pl.when(i >= FIRST)
-        def _():
-            for c in reads(i):
-                c.wait()
-
+    def finish(copies):
+        for c in copies:
+            c.wait()
+
+    def attend(i):
+        kbuf, vbuf, slot, _ = home(i)
         rows = []
         for g in range(2):
             b = 2 * i + g
             pos = pos_ref[b]
             at = pos - base
-            lines = pl.ds(pl.multiple_of(b * heads, heads), heads)
+            lines = pl.ds(b * heads, heads)
             spot = pl.ds(pl.multiple_of(at * heads, heads), heads)
-            ks = 2 * jnp.where(i < HELD, i, place(jnp.maximum(i, HELD))) + g
+            ks = 2 * slot + g
 
             @pl.when(jnp.logical_and(at >= 0, at < span))
             def _():
-                kring[ks, spot, :] = fresh(1, lines)
-                vring[ks, spot, :] = fresh(2, lines)
+                kbuf[ks, spot, :] = fresh(1, lines)
+                vbuf[ks, spot, :] = fresh(2, lines)
 
             rows.append((b, pos, lines, ks))
         scores = []
         for b, pos, lines, ks in rows:
-            score = lax.dot_general(fresh(0, lines), kring[ks], NT, preferred_element_type=F32) * scale
+            score = lax.dot_general(fresh(0, lines), kbuf[ks], NT, preferred_element_type=F32) * scale
             scores.append(jnp.where(slot_of <= pos, score, -jnp.inf))
         for (b, pos, lines, ks), score in zip(rows, scores):
             top = jnp.max(score, axis=-1, keepdims=True)
             safe = jnp.where(top == -jnp.inf, 0.0, top)
             weight = jnp.exp(score - safe)
             total = jnp.sum(weight, axis=-1, keepdims=True)
-            mix = jnp.dot(weight.astype(BF16), vring[ks], preferred_element_type=F32)
+            mix = jnp.dot(weight.astype(BF16), vbuf[ks], preferred_element_type=F32)
             obuf[0, lines, :] = mix[:, :128]
             obuf[1, lines, :] = mix[:, 128:]
             mbuf[lines, :] = jnp.broadcast_to(top, (heads, 128))
             lbuf[lines, :] = jnp.broadcast_to(total, (heads, 128))
 
-        @pl.when(jnp.logical_and(i >= HELD, i < pairs - 1))
-        def _():
-            for c in writes(i):
-                c.start()
-
-        return carry
-
-    lax.fori_loop(0, pairs, body, 0)
+    for what, i in PLAN:
+        if what == "r":
+            begin(reads(i))
+        elif what == "w":
+            begin(writes(i))
+        elif what == "R":
+            finish(reads(i))
+        elif what == "W":
+            finish(writes(i))
+        else:
+            attend(i)
     eye = (lax.broadcasted_iota(jnp.int32, (batch, 128), 0)
            == lax.broadcasted_iota(jnp.int32, (batch, 128), 1))
     me = lax.axis_index("seq")
@@ -215,19 +222,15 @@
                 chunk[line:line + 1, 128:] = jnp.zeros((1, hd - 128), F32)
         used = per * batch + 2 * per
         chunk[used:, :] = jnp.zeros((chunk.shape[0] - used, hd), F32)
-    for i in range(pairs - flow, pairs - 1):
-        for c in writes(i):
-            c.wait()
 
 
 def write_kernel(kring, vring, ko_in, vo_in, chunk, ko_hbm, vo_hbm, done, sem):
     pairs = ko_hbm.shape[0] // 2
-    last = HELD + (pairs - 1 - HELD) % (RING - HELD)
     copies = []
-    for i, slot in [(i, i) for i in range(HELD)] + [(pairs - 1, last)]:
+    for i in range(pairs - KEPT, pairs):
         for src, dst in ((kring, ko_hbm), (vring, vo_hbm)):
             c = pltpu.make_async_copy(
-                src.at[pl.ds(slot * 2, 2)], dst.at[pl.ds(i * 2, 2)], sem.at[len(copies)])
+                src.at[pl.ds(SLOTS[i] * 2, 2)], dst.at[pl.ds(i * 2, 2)], sem.at[len(copies)])
             c.start()
             copies.append(c)
     done[...] = jnp.zeros_like(done)
@@ -276,27 +279,30 @@
         at = pl.multiple_of((2 * j + side) * cols, 128)
         return jnp.dot(attn, wo[:, pl.ds(at, cols)], preferred_element_type=F32)
 
-    for j in range(chips):
-        theirs[j] = product(j, 1 - core)
+    route = [_flip(chip, d) for d in range(chips - 1, -1, -1)]
+    for k, there in enumerate(route):
+        theirs[k] = product(there, 1 - core)
     joined()
-    swap = pltpu.make_async_remote_copy(
-        src_ref=theirs, dst_ref=half, send_sem=s1, recv_sem=r1,
-        device_id=spot(_flip(me, 1)), device_id_type=MESH)
-    swap.start()
-    for j in range(chips):
-        ours[j] = product(j, core)
-    swap.wait_recv()
-    for j in range(chips):
-        ours[j] += half[j]
+    swaps = []
+    for k in range(chips):
+        c = pltpu.make_async_remote_copy(
+            src_ref=theirs.at[k], dst_ref=half.at[k], send_sem=s1.at[k], recv_sem=r1.at[k],
+            device_id=spot(_flip(me, 1)), device_id_type=MESH)
+        c.start()
+        swaps.append(c)
+    for k, there in enumerate(route):
+        ours[k] = product(there, core)
     moves = []
-    for i in range(chips - 1):
-        there = _flip(chip, chips - 1 - i)
-        c = pltpu.make_async_remote_copy(
-            src_ref=ours.at[there], dst_ref=ygot.at[i], send_sem=s2.at[i], recv_sem=r2.at[i],
-            device_id=spot(2 * there + core), device_id_type=MESH)
-        c.start()
-        moves.append(c)
-    acc = ours[chip]
+    for k, there in enumerate(route):
+        swaps[k].wait_recv()
+        ours[k] += half[k]
+        if k < chips - 1:
+            c = pltpu.make_async_remote_copy(
+                src_ref=ours.at[k], dst_ref=ygot.at[k], send_sem=s2.at[k], recv_sem=r2.at[k],
+                device_id=spot(2 * there + core), device_id_type=MESH)
+            c.start()
+            moves.append(c)
+    acc = ours[chips - 1]
     for i in range(chips - 2, -1, -1):
         moves[i].wait_recv()
         acc = acc + ygot[i]
@@ -312,7 +318,7 @@
         c.wait_recv()
     for p in range(ndev):
         y_ref[:, p * cols:(p + 1) * cols] = yout[p]
-    for c in [swap] + moves + shares:
+    for c in swaps + moves + shares:
         c.wait_send()
 
 
@@ -356,12 +362,14 @@
             out_specs=(any_spec, any_spec, vmem, vmem) + (vmem,) * nseq,
             input_output_aliases={4: 2, 5: 3},
             scratch_shapes=[
+                pltpu.VMEM((2 * MORE, span * heads, hd), BF16),
+                pltpu.VMEM((2 * MORE, span * heads, hd), BF16),
                 pltpu.VMEM((2, batch * heads, 128), F32),
                 pltpu.VMEM((batch * heads, 128), F32),
                 pltpu.VMEM((batch * heads, 128), F32),
-                dma((RING,)), dma((RING,)), dma((RING,)), dma((RING,)),
+                dma((RING + MORE,)), dma((RING + MORE,)), dma((RING + MORE,)), dma((RING + MORE,)),
             ],
-            compiler_params=pltpu.CompilerParams(vmem_limit_bytes=4 * 2**20),
+            compiler_params=pltpu.CompilerParams(vmem_limit_bytes=11 * 2**20),
         )(positions, qkv, k_flat, v_flat, kring, vring)
         got = [lax.ppermute(chunks[d], "seq", [(i, i ^ d) for i in range(nseq)]) for d in range(1, nseq)]
         k_out, v_out, after = pl.pallas_call(
@@ -370,7 +378,7 @@
             in_specs=[vmem, vmem, any_spec, any_spec, vmem],
             out_specs=(any_spec, any_spec, vmem),
             input_output_aliases={2: 0, 3: 1},
-            scratch_shapes=[dma((2 * HELD + 2,))],
+            scratch_shapes=[dma((2 * KEPT,))],
             compiler_params=pltpu.CompilerParams(vmem_limit_bytes=1 * 2**20),
             cost_estimate=pl.CostEstimate(flops=10**9, bytes_accessed=2**24, transcendentals=0),
         )(kring, vring, k_out, v_out, chunks[0])
@@ -386,7 +394,7 @@
                 pltpu.VMEM((ndev // 2, batch, ycols), F32),
                 pltpu.VMEM((ndev // 2 - 1, batch, ycols), F32),
                 pltpu.VMEM((ndev, batch, ycols), BF16),
-                dma, dma, dma((ndev // 2 - 1,)), dma((ndev // 2 - 1,)), dma((ndev - 1,)), dma((ndev - 1,)),
+                dma((ndev // 2,)), dma((ndev // 2,)), dma((ndev // 2 - 1,)), dma((ndev // 2 - 1,)), dma((ndev - 1,)), dma((ndev - 1,)),
             ],
             compiler_params=pltpu.CompilerParams(
                 collective_id=1, has_side_effects=True, vmem_limit_bytes=6 * 2**20),

time: 69.7 us -> 64.8 us (0.930)
  Pallas kernels: 66.6 us -> 61.4 us
    pallas_call x1, Pallas kernels: 35.5 us -> 31.8 us  [local_step(): pl.pallas_call(functools.partial(attend_kernel, hd ** (-0.5)), out_shape=...]
    pallas_call x1, Pallas kernels: 12.6 us -> 11.7 us  [local_step(): pl.pallas_call(project_kernel, out_shape=(jax.ShapeDtypeStruct((3, 2, bat...]
  transfers between devices with their start and end apart: 3 -> 3, of which waited for: 0 -> 0; matrix products, arithmetic and copies ran while one was open for 0% -> 0% of each run, Pallas kernels for 9% -> 10%
where the time goes in v4:
time: 64.8 us; the launch traced here: 64.7 us
  Pallas kernels  61.4 us (95%)
  starting transfers between devices  1.88 us (3%)
  between operations  0.71 us (1%)
  local copies, waits for them, and re-layouts  0.69 us (1%)
    pallas_call x1, Pallas kernels, local_step(): pl.pallas_call(functools.partial(attend_kernel, hd ** (-0.5)), out_shape=...  31.8 us
    pallas_call x1, Pallas kernels, local_step(): pl.pallas_call(project_kernel, out_shape=(jax.ShapeDtypeStruct((3, 2, bat...  11.7 us
    pallas_call x1, Pallas kernels, local_step(): pl.pallas_call(finish_kernel, out_shape=jax.ShapeDtypeStruct((batch, mode...  11.6 us
    pallas_call x1, Pallas kernels, local_step(): pl.pallas_call(write_kernel, out_shape=(cache, cache, jax.ShapeDtypeStruc...  6.39 us
    ppermute x3, starting transfers between devices, local_step(): lax.ppermute(chunks[d], 'seq', [(i, i ^ d) for i in range(nseq)])  1.88 us
  transfers between devices with their start and end apart: 3, of which 0 were waited for; matrix products, arithmetic and copies ran while one was open for 0% of the time, Pallas kernels for 10%

profile of v4, /device:TPU:0, one launch (start us, length us, event | category | flops | bytes accessed | tf_op | source)
XLA Modules:
  0.0 64.7 jit_solution(4858153718102706157)
XLA Ops:
  0.6 0.0 copy-start.1
  0.6 11.7 %shard_map.103 = (f32[3,2,256,128]{3,2,1,0:T(8,128)S(1)}, bf16[16,2048,256]{2,1,0:T(8,128)(2,1)S(1)}, bf16[16,2048,256]{2,1,0:T(8,128)(2,1)S(1)}) custom-call(bf16[32,3072]{1,0:T(8,128)(2,1)} %x_hbm.1, bf16[3072,4096]{1,0:T(8,128)(2,1)} %wq_ref.1, bf16[3072,4096]{1,0:T(8,128)(2,1)} %wk_ref.1, bf16[3072,4096]{1,0:T(8,128)(2,1)} %wv_ref.1, ...), custom_call_target="tpu_custom_call" | custom-call | tf_op jit(solution)/shard_map/pallas_call | solution.py:342
  12.3 0.0 copy-done.1
  12.3 31.8 %shard_map.104 = (bf16[32,2048,256]{2,1,0:T(8,128)(2,1)}, bf16[32,2048,256]{2,1,0:T(8,128)(2,1)}, bf16[16,2048,256]{2,1,0:T(8,128)(2,1)S(1)}, bf16[16,2048,256]{...) custom-call(s32[32]{0:T(128)S(1)} %copy-done.1, ...), custom_call_target="tpu_custom_call", output_to_operand_aliasing={{2}: (4, {}), {3}: (5, {})} | custom-call | tf_op jit(solution)/shard_map/pallas_call | solution.py:358
  44.1 0.2 collective-permute-start
  44.3 0.7 %collective-permute-start.1 = (f32[72,256]{1,0:T(8,128)S(1)}, f32[72,256]{1,0:T(8,128)S(1)}, u32[]{:S(2)}, u32[]{:S(2)}) collective-permute-start(f32[72,256]{1,0:T(8,128)S(1)} %get-tuple-element.22), channel_id=1, source_target_pairs={{0,2},{1,3},{2,0},{3,1},{4,6},{5,7},{6,4},{7,5}} | collective-permute-start | bytes 221192 | tf_op jit(solution)/shard_map/ppermute | solution.py:374
  45.0 1.0 %collective-permute-start.2 = (f32[72,256]{1,0:T(8,128)S(1)}, f32[72,256]{1,0:T(8,128)S(1)}, u32[]{:S(2)}, u32[]{:S(2)}) collective-permute-start(f32[72,256]{1,0:T(8,128)S(1)} %get-tuple-element.23), channel_id=1, source_target_pairs={{0,3},{1,2},{2,1},{3,0},{4,7},{5,6},{6,5},{7,4}} | collective-permute-start | bytes 221192 | tf_op jit(solution)/shard_map/ppermute | solution.py:374
  46.0 0.0 copy-start
  46.0 6.4 %shard_map.105 = (bf16[32,2048,256]{2,1,0:T(8,128)(2,1)}, bf16[32,2048,256]{2,1,0:T(8,128)(2,1)}, f32[8,128]{1,0:T(8,128)S(1)}) custom-call(bf16[16,2048,256]{2,1,0:T(8,128)(2,1)S(1)} %get-tuple-element.24.kring, bf16[16,2048,256]{2,1,0:T(8,128)(2,1)S(1)} %get-tuple-element.25.vring, ...), custom_call_target="tpu_custom_call", output_to_operand_aliasing={{0}: (2, {}), {1}: (3, {})} | custom-call | flops 1000000000 | bytes 16777216 | tf_op jit(solution)/shard_map/pallas_call | solution.py:375
  52.4 0.0 collective-permute-done.refs_1_
  52.4 0.0 collective-permute-done.1.refs_2_
  52.4 0.0 collective-permute-done.2.refs_3_
  52.4 0.0 copy-done
  52.4 11.6 %shard_map.106 = bf16[32,3072]{1,0:T(8,128)(2,1)S(1)} custom-call(f32[72,256]{1,0:T(8,128)S(1)} %get-tuple-element.20.chunk.refs_0_, f32[72,256]{1,0:T(8,128)S(1)} %collective-permute-done.refs_1_, f32[72,256]{1,0:T(8,128)S(1)} %collective-permute-done.1.refs_2_, f32[72,256]{1,0:T(8,128)S(1)} %collective-permute-done.2.refs_3_, ...), custom_call_target="tpu_custom_call" | custom-call | tf_op jit(solution)/shard_map/pallas_call | solution.py:386
  64.0 0.7 %copy.20 = bf16[32,3072]{1,0:T(8,128)(2,1)} copy(bf16[32,3072]{1,0:T(8,128)(2,1)S(1)} %shard_map.106) | data formatting | bytes 393216
Async XLA Ops:
  0.6 11.7 %copy-start.1 = (s32[32]{0:T(128)S(1)}, s32[32]{0:T(128)}, u32[]{:S(2)}) copy-start(s32[32]{0:T(128)} %pos_ref.1) | copy-start | bytes 388
  44.1 8.3 %collective-permute-start = (f32[72,256]{1,0:T(8,128)S(1)}, f32[72,256]{1,0:T(8,128)S(1)}, u32[]{:S(2)}, u32[]{:S(2)}) collective-permute-start(f32[72,256]{1,0:T(8,128)S(1)} %get-tuple-element.21), channel_id=1, source_target_pairs={{0,1},{1,0},{2,3},{3,2},{4,5},{5,4},{6,7},{7,6}} | collective-permute-start | bytes 221192 | tf_op jit(solution)/shard_map/ppermute | solution.py:374
  44.3 8.1 %collective-permute-start.1 = (f32[72,256]{1,0:T(8,128)S(1)}, f32[72,256]{1,0:T(8,128)S(1)}, u32[]{:S(2)}, u32[]{:S(2)}) collective-permute-start(f32[72,256]{1,0:T(8,128)S(1)} %get-tuple-element.22), channel_id=1, source_target_pairs={{0,2},{1,3},{2,0},{3,1},{4,6},{5,7},{6,4},{7,5}} | collective-permute-start | bytes 221192 | tf_op jit(solution)/shard_map/ppermute | solution.py:374
  45.0 7.4 %collective-permute-start.2 = (f32[72,256]{1,0:T(8,128)S(1)}, f32[72,256]{1,0:T(8,128)S(1)}, u32[]{:S(2)}, u32[]{:S(2)}) collective-permute-start(f32[72,256]{1,0:T(8,128)S(1)} %get-tuple-element.23), channel_id=1, source_target_pairs={{0,3},{1,2},{2,1},{3,0},{4,7},{5,6},{6,5},{7,4}} | collective-permute-start | bytes 221192 | tf_op jit(solution)/shard_map/ppermute | solution.py:374
  46.0 6.4 %copy-start = (bf16[512,3072]{1,0:T(8,128)(2,1)S(1)}, bf16[512,3072]{1,0:T(8,128)(2,1)}, u32[]{:S(2)}) copy-start(bf16[512,3072]{1,0:T(8,128)(2,1)} %refs_4_.1) | copy-start | bytes 9437188
